TPU v7x, 32 devices: a whole 2x2x4 slice. The times are simulated.
32 devices in a mesh: task: 8 (over z, core), tp: 4 (over y, x).
Axes of the slice: x: 2, y: 2, z: 4, core: 2. Of those that a mesh axis runs over, the one named last changes fastest.
Arguments:
- support_x: bfloat16 [8, 384, 3584], P('task'), may hold values from -6 to 6
- adapter_a: bfloat16 [8, 3584, 64], P('task'), may hold values from -0.09375 to 0.09375
- gate_pre: bfloat16 [8, 384, 10240], P('task', None, 'tp'), may hold values from -6 to 6
- lengths: int32 [8], P('task'), may hold values from 128 to 384, as said below
- damping: float32 [8], P('task'), may hold values from 0.03 to 0.3
- down_w: bfloat16 [10240, 3584], P('tp', 'task'), may hold values from -0.0625 to 0.0625
- grad_b: float32 [8, 64, 10240], P('task', None, 'tp'), may hold values from -6 to 6
Outputs:
- solution: float32 [8, 64, 10240], P('task', None, 'tp')
- residual: float32 [8, 64, 10240], P('task', None, 'tp')
Inputs may be any that keep to these rules, and one draw needn't show every extreme that they name: `lengths`: each a multiple of 128; some task has exactly 384.
All inputs are finite; a program needn't handle non-finite values.
Results may differ from a plain program's by a relative error of at most 0.033.
Values may be sent and summed in bfloat16 or wider, within the bound.
A program may use at most 64 MiB of HBM per device.

v0:
```python
import functools

import jax
import jax.numpy as jnp
from jax import lax
from jax.experimental import pallas as pl
from jax.experimental.pallas import tpu as pltpu
from jax.sharding import PartitionSpec as P

ITERS = 2


def shards(support_x, adapter_a, gate_pre, lengths, damping, down_w, grad_b):
    down_full = lax.all_gather(down_w, "task", axis=1, tiled=True)
    features = jnp.dot(support_x[0], adapter_a[0], preferred_element_type=jnp.float32).astype(
        jnp.bfloat16
    )
    positions = lax.broadcasted_iota(jnp.int32, (gate_pre.shape[1], 1), 0)
    gated = jnp.where(
        positions < lengths[0], jax.nn.silu(gate_pre[0].astype(jnp.float32)), 0.0
    ).astype(jnp.bfloat16)
    tokens_live = lengths[0].astype(jnp.float32)
    damping_rate = damping[0]

    def transposed(mixed_rows):
        return lax.dot_general(
            mixed_rows, down_full, (((1,), (1,)), ((), ())), preferred_element_type=jnp.float32
        )

    def apply(vector):
        inner = jnp.dot(features, vector.astype(jnp.bfloat16), preferred_element_type=jnp.float32)
        active = (gated * inner).astype(jnp.bfloat16)
        partial_sum = jnp.dot(active, down_full, preferred_element_type=jnp.float32)
        mixed = lax.psum(partial_sum.astype(jnp.bfloat16), "tp")
        second = (gated * transposed(mixed)).astype(jnp.bfloat16)
        product = lax.dot_general(
            features, second, (((0,), (0,)), ((), ())), preferred_element_type=jnp.float32
        )
        return product / tokens_live + damping_rate * vector

    def paired_sums(vector, image):
        return lax.psum((jnp.sum(vector * vector), jnp.sum(vector * image)), "tp")

    target = grad_b[0]
    solution = jnp.zeros_like(target)
    residual = target
    image = apply(residual)
    norm_now, product = paired_sums(residual, image)
    alpha = norm_now / product
    direction, along = (residual, image)
    for step in range(ITERS):
        solution = solution + alpha * direction
        residual = residual - alpha * along
        if step + 1 < ITERS:
            image = apply(residual)
            norm_next, product = paired_sums(residual, image)
            ratio = norm_next / norm_now
            alpha = norm_next / (product - ratio * norm_next / alpha)
            direction = residual + ratio * direction
            along = image + ratio * along
            norm_now = norm_next
    return (solution[None], residual[None])


MESH = pl.DeviceIdType.MESH


def kernel(
    n_task, n_tp,
    support_hbm, adapter_hbm, gate_hbm, scal_ref, w_hbm, grad_hbm,
    sol_ref, res_ref,
    support, adapter, grad, weights, gated, active, total, features, image0, image1,
    part1, got1, mixed1, part2, got2, mixed2, sums, sums_got,
    load_sem, w_send, d2d_send, w_recv, rs_send1, rs_recv1, ag_send1, ag_recv1,
    rs_send2, rs_recv2, ag_send2, ag_recv2, fw_send, fw_recv, sum_send, sum_recv,
):
    t_me, j_me = lax.axis_index("task"), lax.axis_index("tp")
    planes = n_task // 2
    z, core = t_me // 2, t_me % 2
    other = 1 - core
    blk = part1.shape[3]
    subs = w_hbm.shape[0] // blk
    hidden = w_hbm.shape[1]
    rows = part1.shape[2]
    tile = next(size for size in (512, 256, 128) if hidden % size == 0)
    n_chunk, chunk = part2.shape[0], part2.shape[3]

    def block(u):
        return weights.at[pl.ds(pl.multiple_of(u * blk, 16), blk)]

    mine_all = weights.at[pl.ds(pl.multiple_of(t_me * subs * blk, 16), subs * blk)]
    own = pltpu.make_async_copy(w_hbm, mine_all, load_sem.at[0])
    own.start()
    loads = [
        pltpu.make_async_copy(source, target, load_sem.at[1 + place])
        for place, (source, target) in enumerate(
            ((gate_hbm, active), (support_hbm, support), (adapter_hbm, adapter), (grad_hbm, grad))
        )
    ]
    for load in loads:
        load.start()

    up, down = {"task": t_me + 2, "tp": j_me}, {"task": t_me - 2, "tp": j_me}
    partner = {"task": 2 * z + other, "tp": j_me}
    peers = [{"task": t_me, "tp": lax.rem(j_me + d, n_tp)} for d in range(1, n_tp)]

    barrier = pltpu.get_barrier_semaphore()
    for peer in [partner] + peers:
        pl.semaphore_signal(barrier, inc=1, device_id=peer, device_id_type=MESH)

    @pl.when(z < planes - 1)
    def _():
        pl.semaphore_signal(barrier, inc=1, device_id=up, device_id_type=MESH)

    @pl.when(z > 0)
    def _():
        pl.semaphore_signal(barrier, inc=1, device_id=down, device_id_type=MESH)

    pl.semaphore_wait(barrier, n_tp + lax.min(z, 1) + lax.min(planes - 1 - z, 1))
    own.wait()

    def send_block(t, target, send_sem):
        return pltpu.make_async_remote_copy(
            src_ref=block(t), dst_ref=block(t), send_sem=send_sem, recv_sem=w_recv.at[t],
            device_id=target, device_id_type=MESH,
        )

    def arrived(t):
        pltpu.make_async_copy(block(t), block(t), w_recv.at[t]).wait()

    def pass_on(plane, s, d, from_left):
        t = (2 * plane + core) * subs + s

        @pl.when(d > 0)
        def _():
            arrived(t)

        if from_left:
            @pl.when(z < planes - 1)
            def _():
                send_block(t, up, w_send.at[0, t]).start()

        @pl.when((z > 0) & ((d == 0) | (not from_left)))
        def _():
            send_block(t, down, w_send.at[1, t]).start()

        send_block(t, partner, d2d_send.at[t]).start()

    for s in range(subs):
        pass_on(z, s, 0, True)

    loads[1].wait()
    loads[2].wait()
    features[...] = jnp.dot(
        support[...], adapter[...], preferred_element_type=jnp.float32
    ).astype(jnp.bfloat16)
    loads[0].wait()
    live, rate = scal_ref[0:1, 0:1], scal_ref[1:2, 0:1]
    tokens = active.shape[0]
    positions = lax.broadcasted_iota(jnp.int32, (tokens, tile), 0).astype(jnp.float32)

    def columns(i):
        return pl.ds(pl.multiple_of(i * tile, tile), tile)

    @pl.loop(0, hidden // tile)
    def _(i):
        pre = active[:, columns(i)].astype(jnp.float32)
        gated[:, columns(i)] = jnp.where(
            positions < live, pre / (1.0 + jnp.exp(-pre)), 0.0
        ).astype(jnp.bfloat16)

    loads[3].wait()

    def make_active(vector):
        @pl.loop(0, hidden // tile)
        def _(i):
            inner = jnp.dot(
                features[...], vector[:, columns(i)].astype(jnp.bfloat16),
                preferred_element_type=jnp.float32,
            )
            active[:, columns(i)] = (gated[:, columns(i)].astype(jnp.float32) * inner).astype(
                jnp.bfloat16
            )
            total[:, columns(i)] = jnp.zeros_like(inner)

    def product(which, first, size, part, got, send_sem, recv_sem):
        span = pl.ds(pl.multiple_of(first, 16), size)
        partial_sum = lax.dot_general(
            active[...], weights[span, :], (((1,), (1,)), ((), ())),
            preferred_element_type=jnp.float32,
        )
        part[which] = partial_sum.astype(jnp.bfloat16).reshape(n_tp, rows, size)
        for d in range(1, n_tp):
            pltpu.make_async_remote_copy(
                src_ref=part.at[which, lax.rem(j_me + d, n_tp)], dst_ref=got.at[which, d - 1],
                send_sem=send_sem.at[which], recv_sem=recv_sem.at[which],
                device_id=peers[d - 1], device_id_type=MESH,
            ).start()

    def reduce(which, part, got, mixed, recv_sem, send_sem, out_sem, targets):
        pltpu.make_async_copy(got.at[which], got.at[which], recv_sem.at[which]).wait()
        added = part[which, j_me].astype(jnp.float32)
        for d in range(1, n_tp):
            added = added + got[which, d - 1].astype(jnp.float32)
        mixed[which, j_me] = added.astype(jnp.bfloat16)
        for target in targets:
            pltpu.make_async_remote_copy(
                src_ref=mixed.at[which, j_me], dst_ref=mixed.at[which, j_me],
                send_sem=send_sem.at[which], recv_sem=out_sem.at[which],
                device_id=target, device_id_type=MESH,
            ).start()

    def back(which, first, size, mixed):
        span = pl.ds(pl.multiple_of(first, 16), size)
        whole = mixed[which].reshape(n_tp * rows, size)

        @pl.loop(0, hidden // tile)
        def _(i):
            total[:, columns(i)] += jnp.dot(
                whole, weights[span, columns(i)], preferred_element_type=jnp.float32
            )

    def make_image(vector, image, slot):
        def body(i, carry):
            second = (gated[:, columns(i)].astype(jnp.float32) * total[:, columns(i)]).astype(
                jnp.bfloat16
            )
            outer = lax.dot_general(
                features[...], second, (((0,), (0,)), ((), ())),
                preferred_element_type=jnp.float32,
            )
            v = vector[:, columns(i)]
            value = outer / live + rate * v
            image[:, columns(i)] = value
            return carry[0] + v * v, carry[1] + v * value

        zero = jnp.zeros((vector.shape[0], tile), jnp.float32)
        squares, crosses = lax.fori_loop(0, hidden // tile, body, (zero, zero))
        sums[slot, 0] = jnp.broadcast_to(jnp.sum(squares, keepdims=True), (8, 128))
        sums[slot, 1] = jnp.broadcast_to(jnp.sum(crosses, keepdims=True), (8, 128))
        for d in range(1, n_tp):
            pltpu.make_async_remote_copy(
                src_ref=sums.at[slot], dst_ref=sums_got.at[slot, d - 1],
                send_sem=sum_send.at[slot], recv_sem=sum_recv.at[slot],
                device_id=peers[d - 1], device_id_type=MESH,
            ).start()
        got = sums_got.at[slot]
        pltpu.make_async_copy(got, got, sum_recv.at[slot]).wait()
        norm, cross = sums[slot, 0, 0:1, 0:1], sums[slot, 1, 0:1, 0:1]
        for d in range(1, n_tp):
            norm = norm + sums_got[slot, d - 1, 0, 0:1, 0:1]
            cross = cross + sums_got[slot, d - 1, 1, 0:1, 0:1]
        return norm, cross

    make_active(grad)

    @pl.loop(0, planes * subs)
    def _(e):
        d, s = e // subs, e % subs
        left, right = z - d, z + d

        @pl.when((d > 0) & (left >= 0))
        def _():
            pass_on(left, s, d, True)

        @pl.when((d > 0) & (right < planes))
        def _():
            pass_on(right, s, d, False)

        for stage in range(3):
            for plane, there in ((left, left >= 0), (right, (d > 0) & (right < planes))):
                for side in (core, other):
                    @pl.when(there)
                    def _(plane=plane, side=side, mine=side is core, stage=stage):
                        t = (2 * plane + side) * subs + s
                        if stage == 0:
                            if not mine:
                                arrived(t)
                            product(t, t * blk, blk, part1, got1, rs_send1, rs_recv1)
                        elif stage == 1:
                            reduce(t, part1, got1, mixed1, rs_recv1, ag_send1, ag_recv1, peers)
                        else:
                            pieces = mixed1.at[t, pl.ds(0, n_tp - 1)]
                            pltpu.make_async_copy(pieces, pieces, ag_recv1.at[t]).wait()
                            back(t, t * blk, blk, mixed1)

    norm0, cross0 = make_image(grad, image0, 0)
    alpha0 = norm0 / cross0

    @pl.loop(0, hidden // tile)
    def _(i):
        res_ref[:, columns(i)] = grad[:, columns(i)] - alpha0 * image0[:, columns(i)]

    make_active(res_ref)

    @pl.loop(0, n_chunk)
    def _(k):
        product(k, k * chunk, chunk, part2, got2, rs_send2, rs_recv2)

    row, col = j_me // 2, j_me % 2
    beside, below = 2 * row + 1 - col, 2 * (1 - row) + col
    half = rows // 2
    near = [{"task": t_me, "tp": beside}, {"task": t_me, "tp": below}]

    @pl.loop(0, n_chunk)
    def _(k):
        reduce(k, part2, got2, mixed2, rs_recv2, ag_send2, ag_recv2, near)

    def finish(k):
        piece = mixed2.at[k, 0]
        pltpu.make_async_copy(piece, piece, fw_recv.at[k]).wait()
        back(k, k * chunk, chunk, mixed2)

    @pl.loop(0, n_chunk)
    def _(k):
        pieces = mixed2.at[k, pl.ds(0, 2)]
        pltpu.make_async_copy(pieces, pieces, ag_recv2.at[k]).wait()
        for source, start, target in ((beside, 0, near[1]), (below, half, near[0])):
            piece = mixed2.at[k, source, pl.ds(start, half)]
            pltpu.make_async_remote_copy(
                src_ref=piece, dst_ref=piece, send_sem=fw_send.at[k], recv_sem=fw_recv.at[k],
                device_id=target, device_id_type=MESH,
            ).start()

        @pl.when(k > 0)
        def _():
            finish(k - 1)

    finish(n_chunk - 1)

    norm1, cross1 = make_image(res_ref, image1, 1)
    ratio = norm1 / norm0
    alpha1 = norm1 / (cross1 - ratio * norm1 / alpha0)

    @pl.loop(0, hidden // tile)
    def _(i):
        first, then = grad[:, columns(i)], res_ref[:, columns(i)]
        sol_ref[:, columns(i)] = alpha0 * first + alpha1 * (then + ratio * first)
        res_ref[:, columns(i)] = then - alpha1 * (
            image1[:, columns(i)] + ratio * image0[:, columns(i)]
        )

    def drained(ref, sem):
        pltpu.make_async_copy(ref, ref, sem).wait()

    @pl.loop(0, n_task * subs)
    def _(t):
        task = t // subs

        @pl.when((task % 2 == core) & (task // 2 <= z) & (z < planes - 1))
        def _():
            drained(block(t), w_send.at[0, t])

        @pl.when((task % 2 == core) & (task // 2 >= z) & (z > 0))
        def _():
            drained(block(t), w_send.at[1, t])

        @pl.when(task % 2 == core)
        def _():
            drained(block(t), d2d_send.at[t])

        drained(got1.at[t], rs_send1.at[t])
        drained(got1.at[t], ag_send1.at[t])

    @pl.loop(0, n_chunk)
    def _(k):
        drained(got2.at[k], rs_send2.at[k])
        drained(mixed2.at[k, pl.ds(0, 2)], ag_send2.at[k])
        drained(mixed2.at[k, 0], fw_send.at[k])

    for slot in range(2):
        drained(sums_got.at[slot], sum_send.at[slot])


def fused(n_task, n_tp, support_x, adapter_a, gate_pre, lengths, damping, down_w, grad_b):
    tokens, width = support_x.shape[1:]
    rank = adapter_a.shape[2]
    hidden, share = down_w.shape
    blk = share // 2 if share % 32 == 0 else share
    n_block = n_task * share // blk
    rows = tokens // n_tp
    chunk = next(size for size in (512, 256, 128) if width % size == 0)
    n_chunk = width // chunk
    scal = jnp.broadcast_to(
        jnp.concatenate([lengths.astype(jnp.float32), damping])[:, None], (2, 128)
    )
    f32, bf16 = jnp.float32, jnp.bfloat16
    dma = pltpu.SemaphoreType.DMA
    anywhere, vmem = pl.BlockSpec(memory_space=pl.ANY), pl.BlockSpec(memory_space=pltpu.VMEM)
    shape = jax.ShapeDtypeStruct((rank, hidden), f32)
    solved, residual = pl.pallas_call(
        functools.partial(kernel, n_task, n_tp),
        out_shape=(shape, shape),
        in_specs=[anywhere, anywhere, anywhere, vmem, anywhere, anywhere],
        out_specs=(vmem, vmem),
        scratch_shapes=[
            pltpu.VMEM((tokens, width), bf16),
            pltpu.VMEM((width, rank), bf16),
            pltpu.VMEM((rank, hidden), f32),
            pltpu.VMEM((width, hidden), bf16),
            pltpu.VMEM((tokens, hidden), bf16),
            pltpu.VMEM((tokens, hidden), bf16),
            pltpu.VMEM((tokens, hidden), f32),
            pltpu.VMEM((tokens, rank), bf16),
            pltpu.VMEM((rank, hidden), f32),
            pltpu.VMEM((rank, hidden), f32),
            pltpu.VMEM((n_block, n_tp, rows, blk), bf16),
            pltpu.VMEM((n_block, n_tp - 1, rows, blk), bf16),
            pltpu.VMEM((n_block, n_tp, rows, blk), bf16),
            pltpu.VMEM((n_chunk, n_tp, rows, chunk), bf16),
            pltpu.VMEM((n_chunk, n_tp - 1, rows, chunk), bf16),
            pltpu.VMEM((n_chunk, n_tp, rows, chunk), bf16),
            pltpu.VMEM((2, 2, 8, 128), f32),
            pltpu.VMEM((2, n_tp - 1, 2, 8, 128), f32),
            dma((5,)),
            dma((2, n_block)),
            dma((n_block,)),
            dma((n_block,)),
            dma((n_block,)),
            dma((n_block,)),
            dma((n_block,)),
            dma((n_block,)),
            dma((n_chunk,)),
            dma((n_chunk,)),
            dma((n_chunk,)),
            dma((n_chunk,)),
            dma((n_chunk,)),
            dma((n_chunk,)),
            dma((2,)),
            dma((2,)),
        ],
        compiler_params=pltpu.CompilerParams(
            collective_id=0, has_side_effects=True, vmem_limit_bytes=66_000_000
        ),
    )(support_x[0], adapter_a[0], gate_pre[0], scal, down_w.T, grad_b[0])
    return solved[None], residual[None]


def solution(mesh):
    in_specs = (
        P("task", None, None),
        P("task", None, None),
        P("task", None, "tp"),
        P("task"),
        P("task"),
        P("tp", "task"),
        P("task", None, "tp"),
    )
    out_specs = (P("task", None, "tp"), P("task", None, "tp"))
    n_task, n_tp = mesh.shape["task"], mesh.shape["tp"]

    def body(support_x, *rest):
        if n_tp != 4 or support_x.shape[1] % (32 * n_tp):
            return shards(support_x, *rest)
        return fused(n_task, n_tp, support_x, *rest)

    return jax.shard_map(body, mesh=mesh, in_specs=in_specs, out_specs=out_specs, check_vma=False)
```

profile of v0, /device:TPU:0, one launch (start us, length us, event | category | flops | bytes accessed | tf_op | source)
XLA Modules:
  0.0 255.7 jit_solution(10908779178216266176)
XLA Ops:
  1.9 0.1 pad_maximum_fusion
  2.0 0.6 broadcast_in_dim.12.scal_ref
  2.6 2.3 copy.9
  4.9 246.8 %shard_map.86 = (f32[64,2560]{1,0:T(8,128)}, f32[64,2560]{1,0:T(8,128)}) custom-call(bf16[384,3584]{1,0:T(8,128)(2,1)} %bitcast.8, bf16[3584,64]{1,0:T(8,128)(2,1)} %bitcast.7, bf16[384,2560]{1,0:T(8,128)(2,1)} %bitcast.10, f32[2,128]{1,0:T(2,128)} %broadcast_in_dim.12.scal_ref, bf16[448,2560]{1,0:T(8,128)(2,1)} %bitcast.9, f32[64,2560]{1,0:T(8,128)} %bitcast.11), custom_call_target="tpu_custom_call" | custom-call | tf_op jit(solution)/shard_map/pallas_call | solution.py:391
  251.7 2.0 copy.14
  253.7 2.0 copy.15
where the time goes:
time: 256 us
  Pallas kernels  247 us (96%)
  local copies, waits for them, and re-layouts  6.84 us (3%)
    pallas_call x1, Pallas kernels, fused(): pl.pallas_call(functools.partial(kernel, n_task, n_tp), out_shape=(shape,...  247 us
    unnamed x3, local copies, waits for them, and re-layouts  6.2 us

commit v1 on v0

v1 whole, which is shorter than its diff:
```python
import jax
import jax.numpy as jnp
from jax import lax
from jax.experimental import pallas as pl
from jax.experimental.pallas import tpu as pltpu
from jax.sharding import PartitionSpec as P

ITERS = 2


def shards(support_x, adapter_a, gate_pre, lengths, damping, down_w, grad_b):
    down_full = lax.all_gather(down_w, "task", axis=1, tiled=True)
    features = jnp.dot(support_x[0], adapter_a[0], preferred_element_type=jnp.float32).astype(
        jnp.bfloat16
    )
    positions = lax.broadcasted_iota(jnp.int32, (gate_pre.shape[1], 1), 0)
    gated = jnp.where(
        positions < lengths[0], jax.nn.silu(gate_pre[0].astype(jnp.float32)), 0.0
    ).astype(jnp.bfloat16)
    tokens_live = lengths[0].astype(jnp.float32)
    damping_rate = damping[0]

    def transposed(mixed_rows):
        return lax.dot_general(
            mixed_rows, down_full, (((1,), (1,)), ((), ())), preferred_element_type=jnp.float32
        )

    def apply(vector):
        inner = jnp.dot(features, vector.astype(jnp.bfloat16), preferred_element_type=jnp.float32)
        active = (gated * inner).astype(jnp.bfloat16)
        partial_sum = jnp.dot(active, down_full, preferred_element_type=jnp.float32)
        mixed = lax.psum(partial_sum.astype(jnp.bfloat16), "tp")
        second = (gated * transposed(mixed)).astype(jnp.bfloat16)
        product = lax.dot_general(
            features, second, (((0,), (0,)), ((), ())), preferred_element_type=jnp.float32
        )
        return product / tokens_live + damping_rate * vector

    def paired_sums(vector, image):
        return lax.psum((jnp.sum(vector * vector), jnp.sum(vector * image)), "tp")

    target = grad_b[0]
    solution = jnp.zeros_like(target)
    residual = target
    image = apply(residual)
    norm_now, product = paired_sums(residual, image)
    alpha = norm_now / product
    direction, along = (residual, image)
    for step in range(ITERS):
        solution = solution + alpha * direction
        residual = residual - alpha * along
        if step + 1 < ITERS:
            image = apply(residual)
            norm_next, product = paired_sums(residual, image)
            ratio = norm_next / norm_now
            alpha = norm_next / (product - ratio * norm_next / alpha)
            direction = residual + ratio * direction
            along = image + ratio * along
            norm_now = norm_next
    return (solution[None], residual[None])


MESH = pl.DeviceIdType.MESH
HALF = 64
UNIT = 2 * HALF
CHUNK = 256
AHEAD = 3
EARLY = 3


def arrival_order(subs):
    near, far = list(range(subs)), list(range(subs - 1, -1, -1))
    gate = subs
    clock, times = 0.0, []
    for place in near:
        if place == AHEAD:
            clock += gate
        clock += 1.0
        times.append((clock, place))
    events = [(when, 0, place) for when, place in times]
    events += [(place + 1.0, 1, 2 * subs + far[place]) for place in near]
    clock = float(subs)
    for when, place in times:
        clock = max(clock, when) + 1.0
        events.append((clock, 2, 3 * subs + far[place]))
    middle = [subs + place for place in near] + [unit for _, _, unit in sorted(events)]
    end = near + [subs + place for place in near] + [2 * subs + place for place in far]
    return end + [0] * subs, middle


def kernel(
    support_hbm, adapter_hbm, gate_hbm, length_ref, damping_ref, w_hbm, grad_hbm,
    sol_ref, res_ref,
    support, adapter, grad, weights, gated, active, total, features, image0, image1,
    far_gated, far_active, far_total, far_features, vector16, far_vector, far_image, image_got,
    part1, got1, mixed1, part2, pass2, added2, got2, mixed2, sums, sums_got,
    load_sem, w_recv, p_recv, in_send, out_send, d2d_send, far_send, far_recv,
    rs_send1, rs_recv1, ag_send1, ag_recv1, rs_send2, pass_recv2, rs_recv2,
    ag_send2, ag_recv2, fw_send, fw_recv, sum_send, sum_recv,
):
    t_me, j_me = lax.axis_index("task"), lax.axis_index("tp")
    z, core = t_me // 2, t_me % 2
    other = 1 - core
    upper = z // 2
    inner = z + upper * (3 - 2 * z)
    n_tp, rows = part1.shape[1:3]
    tokens, hidden = active.shape
    width = weights.shape[0]
    subs = w_hbm.shape[0] // HALF
    n_unit = 4 * subs
    n_chunk = part2.shape[0]
    tile = far_image.shape[2]
    n_tile = hidden // tile
    orders = arrival_order(subs)

    def unit_of(e):
        unit = orders[0][0] + inner * (orders[1][0] - orders[0][0])
        for place in range(1, n_unit):
            first, second = orders[0][place], orders[1][place]
            unit = jnp.where(e == place, first + inner * (second - first), unit)
        return unit

    def placed(p):
        return p + upper * (n_unit - 1 - 2 * p)

    def half(p, side):
        return weights.at[pl.ds(pl.multiple_of(placed(p) * UNIT + side * HALF, HALF), HALF)]

    def span(p):
        return pl.ds(pl.multiple_of(placed(p) * UNIT, UNIT), UNIT)

    own = [
        pltpu.make_async_copy(
            w_hbm.at[pl.ds(s * HALF, HALF)],
            weights.at[pl.ds(pl.multiple_of((z * subs + s) * UNIT + core * HALF, HALF), HALF)],
            load_sem.at[0],
        )
        for s in range(subs)
    ]
    for load in own:
        load.start()
    loads = [
        pltpu.make_async_copy(source, target, load_sem.at[1 + place])
        for place, (source, target) in enumerate(
            ((gate_hbm, active), (support_hbm, support), (adapter_hbm, adapter), (grad_hbm, grad))
        )
    ]
    for load in loads:
        load.start()

    inward = {"task": t_me + 2 - 4 * upper, "tp": j_me}
    outward = {"task": t_me - 2 + 4 * upper, "tp": j_me}
    partner = {"task": 2 * z + other, "tp": j_me}
    peers = [{"task": t_me, "tp": lax.rem(j_me + d, n_tp)} for d in range(1, n_tp)]

    barrier = pltpu.get_barrier_semaphore()
    for peer in [partner, inward] + peers:
        pl.semaphore_signal(barrier, inc=1, device_id=peer, device_id_type=MESH)

    @pl.when(inner == 1)
    def _():
        pl.semaphore_signal(barrier, inc=1, device_id=outward, device_id_type=MESH)

    pl.semaphore_wait(barrier, n_tp + 1 + inner)

    def drained(ref, sem):
        pltpu.make_async_copy(ref, ref, sem).wait()

    def push(src, dst, send_sem, recv_sem, target):
        pltpu.make_async_remote_copy(
            src_ref=src, dst_ref=dst, send_sem=send_sem, recv_sem=recv_sem,
            device_id=target, device_id_type=MESH,
        ).start()

    def send_half(p, target, send_sem):
        push(half(p, core), half(p, core), send_sem.at[0], w_recv.at[placed(p)], target)

    def share_half(p):
        push(half(p, core), half(p, core), d2d_send.at[0], p_recv.at[placed(p)], partner)

    def arrive(p):
        drained(half(p, core), w_recv.at[placed(p)])

        @pl.when((inner == 1) & (p < subs))
        def _():
            send_half(p, inward, in_send)

        @pl.when((inner == 1) & (p >= 2 * subs) & ((p < 3 * subs) | (p >= n_unit - EARLY)))
        def _():
            send_half(p, outward, out_send)

        share_half(p)

    def completed(p):
        drained(half(p, other), p_recv.at[placed(p)])

    first = inner * subs
    drained(weights.at[pl.ds(0, subs * HALF)], load_sem.at[0])

    @pl.loop(0, AHEAD)
    def _(s):
        send_half(first + s, inward, in_send)

        @pl.when(inner == 1)
        def _():
            send_half(first + s, outward, out_send)

        share_half(first + s)

    @pl.when(inner == 1)
    def _():
        @pl.loop(AHEAD, subs)
        def _(s):
            send_half(first + s, inward, in_send)
            send_half(first + s, outward, out_send)

    @pl.loop(AHEAD, subs)
    def _(s):
        share_half(first + s)

    loads[1].wait()
    loads[2].wait()
    features[...] = lax.dot_general(
        support[...], adapter[...], (((1,), (1,)), ((), ())), preferred_element_type=jnp.float32
    ).astype(jnp.bfloat16)
    loads[0].wait()
    loads[3].wait()
    live, rate = length_ref[0].astype(jnp.float32), damping_ref[0]
    positions = lax.broadcasted_iota(jnp.int32, (tokens, tile), 0).astype(jnp.float32)

    def columns(i):
        return pl.ds(pl.multiple_of(i * tile, tile), tile)

    @pl.loop(0, n_tile)
    def _(i):
        pre = active[:, columns(i)].astype(jnp.float32)
        gated[:, columns(i)] = jnp.where(
            positions < live, pre / (1.0 + jnp.exp(-pre)), 0.0
        ).astype(jnp.bfloat16)
        vector16[:, columns(i)] = grad[:, columns(i)].astype(jnp.bfloat16)

    @pl.when(inner == 0)
    def _():
        for place, (src, dst) in enumerate(
            ((features, far_features), (vector16, far_vector), (gated, far_gated))
        ):
            push(src, dst, far_send.at[place], far_recv.at[place], inward)

        @pl.loop(AHEAD, subs)
        def _(s):
            send_half(first + s, inward, in_send)

    @pl.when(inner == 1)
    def _():
        image_got[...] = jnp.zeros_like(image_got)

    def make_active(feats, vector, gate, act, tot):
        @pl.loop(0, n_tile)
        def _(i):
            wide = jnp.dot(
                feats[...], vector[:, columns(i)], preferred_element_type=jnp.float32
            )
            act[:, columns(i)] = (gate[:, columns(i)].astype(jnp.float32) * wide).astype(
                jnp.bfloat16
            )
            tot[:, columns(i)] = jnp.zeros_like(wide)

    def product(slot, p, act):
        partial_sum = lax.dot_general(
            act[...], weights[span(p), :], (((1,), (1,)), ((), ())),
            preferred_element_type=jnp.float32,
        )
        part1[slot] = partial_sum.astype(jnp.bfloat16).reshape(n_tp, rows, UNIT)
        for d in range(1, n_tp):
            push(
                part1.at[slot, lax.rem(j_me + d, n_tp)], got1.at[slot, d - 1],
                rs_send1.at[0], rs_recv1.at[slot], peers[d - 1],
            )

    def reduce(slot):
        drained(got1.at[slot], rs_recv1.at[slot])
        added = part1[slot, j_me].astype(jnp.float32)
        for d in range(1, n_tp):
            added = added + got1[slot, d - 1].astype(jnp.float32)
        mixed1[slot, j_me] = added.astype(jnp.bfloat16)
        for peer in peers:
            push(
                mixed1.at[slot, j_me], mixed1.at[slot, j_me],
                ag_send1.at[0], ag_recv1.at[slot], peer,
            )

    def back(slot, p, tot):
        drained(mixed1.at[slot, pl.ds(0, n_tp - 1)], ag_recv1.at[slot])
        whole = mixed1[slot].reshape(tokens, UNIT)

        @pl.loop(0, n_tile)
        def _(i):
            tot[:, columns(i)] += jnp.dot(
                whole, weights[span(p), columns(i)], preferred_element_type=jnp.float32
            )

    def make_image(vector, image, slot, extra):
        def body(i, carry):
            second = (gated[:, columns(i)].astype(jnp.float32) * total[:, columns(i)]).astype(
                jnp.bfloat16
            )
            outer = lax.dot_general(
                features[...], second, (((0,), (0,)), ((), ())),
                preferred_element_type=jnp.float32,
            )
            if extra is not None:
                outer = outer + extra[i].astype(jnp.float32)
            v = vector[:, columns(i)]
            value = outer / live + rate * v
            image[:, columns(i)] = value
            return carry[0] + v * v, carry[1] + v * value

        zero = jnp.zeros((vector.shape[0], tile), jnp.float32)
        squares, crosses = lax.fori_loop(0, n_tile, body, (zero, zero))
        sums[slot, 0] = jnp.broadcast_to(jnp.sum(squares, keepdims=True), (8, 128))
        sums[slot, 1] = jnp.broadcast_to(jnp.sum(crosses, keepdims=True), (8, 128))
        for d in range(1, n_tp):
            push(
                sums.at[slot], sums_got.at[slot, d - 1],
                sum_send.at[slot], sum_recv.at[slot], peers[d - 1],
            )
        drained(sums_got.at[slot], sum_recv.at[slot])
        norm, cross = sums[slot, 0, 0:1, 0:1], sums[slot, 1, 0:1, 0:1]
        for d in range(1, n_tp):
            norm = norm + sums_got[slot, d - 1, 0, 0:1, 0:1]
            cross = cross + sums_got[slot, d - 1, 1, 0:1, 0:1]
        return norm, cross

    make_active(features, vector16, gated, active, total)
    count = n_unit - subs + inner * subs

    @pl.loop(0, count + 2)
    def _(e):
        p, before, earlier = unit_of(e), unit_of(e - 1), unit_of(e - 2)

        @pl.when((e >= 1) & (e <= count))
        def _():
            reduce(e - 1)

            @pl.when(before >= 3 * subs)
            def _():
                reduce(before + subs)

        @pl.when(e >= 2)
        def _():
            @pl.when(earlier >= 3 * subs)
            def _():
                back(earlier + subs, earlier, far_total)

            back(e - 2, earlier, total)

        @pl.when(e < count)
        def _():
            @pl.when(e >= subs)
            def _():
                arrive(p)

            completed(p)

            @pl.when(p >= 3 * subs)
            def _():
                @pl.when(p == n_unit - 1)
                def _():
                    for place, ref in enumerate((far_features, far_vector, far_gated)):
                        drained(ref, far_recv.at[place])
                    make_active(far_features, far_vector, far_gated, far_active, far_total)

                product(p + subs, p, far_active)

            product(e, p, active)

    @pl.when(inner == 1)
    def _():
        @pl.loop(0, n_tile)
        def _(i):
            second = (
                far_gated[:, columns(i)].astype(jnp.float32) * far_total[:, columns(i)]
            ).astype(jnp.bfloat16)
            far_image[i] = lax.dot_general(
                far_features[...], second, (((0,), (0,)), ((), ())),
                preferred_element_type=jnp.float32,
            ).astype(jnp.bfloat16)
            push(far_image.at[i], image_got.at[i], far_send.at[3], far_recv.at[3], outward)

        @pl.loop(0, subs - EARLY)
        def _(s):
            send_half(n_unit - 1 - EARLY - s, outward, out_send)

    @pl.when(inner == 0)
    def _():
        @pl.loop(0, EARLY)
        def _(s):
            arrive(n_unit - 1 - s)

        drained(image_got, far_recv.at[3])

    norm0, cross0 = make_image(grad, image0, 0, image_got)
    alpha0 = norm0 / cross0

    @pl.loop(0, n_tile)
    def _(i):
        value = grad[:, columns(i)] - alpha0 * image0[:, columns(i)]
        res_ref[:, columns(i)] = value
        wide = jnp.dot(
            features[...], value.astype(jnp.bfloat16), preferred_element_type=jnp.float32
        )
        active[:, columns(i)] = (gated[:, columns(i)].astype(jnp.float32) * wide).astype(
            jnp.bfloat16
        )
        total[:, columns(i)] = jnp.zeros_like(wide)

    row, col = j_me // 2, j_me % 2
    beside, below = 2 * row + 1 - col, 2 * (1 - row) + col
    across = n_tp - 1 - j_me
    top, low = pl.ds(0, rows // 2), pl.ds(rows // 2, rows // 2)
    side, under = {"task": t_me, "tp": beside}, {"task": t_me, "tp": below}
    early = 3 * subs * UNIT // CHUNK

    def stretch(i):
        c = jnp.where(i < early, i, n_chunk - 1 + early - i)
        start = c * CHUNK + upper * (width - CHUNK - 2 * c * CHUNK)
        return c, pl.ds(pl.multiple_of(start, CHUNK), CHUNK)

    def product2(i):
        c, where = stretch(i)

        @pl.when((inner == 0) & (i >= early))
        def _():
            for p in (2 * c + 1, 2 * c):
                @pl.when(p >= 3 * subs)
                def _(p=p):
                    @pl.when(p < n_unit - EARLY)
                    def _():
                        arrive(p)

                    completed(p)

        partial_sum = lax.dot_general(
            active[...], weights[where, :], (((1,), (1,)), ((), ())),
            preferred_element_type=jnp.float32,
        )
        part2[i] = partial_sum.astype(jnp.bfloat16).reshape(n_tp, rows, CHUNK)
        push(part2.at[i, across, top], pass2.at[i, 0], rs_send2.at[0], pass_recv2.at[i], side)
        push(part2.at[i, across, low], pass2.at[i, 1], rs_send2.at[0], pass_recv2.at[i], under)
        push(part2.at[i, beside, top], got2.at[i, 0, 0], rs_send2.at[0], rs_recv2.at[i], side)
        push(part2.at[i, below, low], got2.at[i, 1, 1], rs_send2.at[0], rs_recv2.at[i], under)

    def relay(i):
        drained(pass2.at[i], pass_recv2.at[i])
        for place, piece, where, target in ((0, below, top, under), (1, beside, low, side)):
            added2[i, place] = (
                part2[i, piece, where].astype(jnp.float32) + pass2[i, place].astype(jnp.float32)
            ).astype(jnp.bfloat16)
            push(
                added2.at[i, place], got2.at[i, 1 - place, place],
                rs_send2.at[0], rs_recv2.at[i], target,
            )

    def reduce2(i):
        drained(got2.at[i], rs_recv2.at[i])
        for place, where in ((0, top), (1, low)):
            mixed2[i, j_me, where] = (
                part2[i, j_me, where].astype(jnp.float32)
                + got2[i, 0, place].astype(jnp.float32)
                + got2[i, 1, place].astype(jnp.float32)
            ).astype(jnp.bfloat16)
        for target in (side, under):
            push(
                mixed2.at[i, j_me], mixed2.at[i, j_me],
                ag_send2.at[0], ag_recv2.at[i], target,
            )

    def forward2(i):
        drained(mixed2.at[i, pl.ds(0, 2)], ag_recv2.at[i])
        for source, where, target in ((beside, top, under), (below, low, side)):
            piece = mixed2.at[i, source, where]
            push(piece, piece, fw_send.at[0], fw_recv.at[i], target)

    def back2(i):
        _, where = stretch(i)
        drained(mixed2.at[i, 0], fw_recv.at[i])
        whole = mixed2[i].reshape(tokens, CHUNK)

        @pl.loop(0, n_tile)
        def _(k):
            total[:, columns(k)] += jnp.dot(
                whole, weights[where, columns(k)], preferred_element_type=jnp.float32
            )

    for start, stop in ((0, early), (early, n_chunk)):
        @pl.loop(start, stop)
        def _(i):
            product2(i)

        @pl.loop(start, stop)
        def _(i):
            relay(i)

        @pl.loop(start, stop)
        def _(i):
            reduce2(i)

    @pl.loop(0, n_chunk + 2)
    def _(i):
        @pl.when(i < n_chunk)
        def _():
            forward2(i)

        @pl.when(i >= 2)
        def _():
            back2(i - 2)

    norm1, cross1 = make_image(res_ref, image1, 1, None)
    ratio = norm1 / norm0
    alpha1 = norm1 / (cross1 - ratio * norm1 / alpha0)

    @pl.loop(0, n_tile)
    def _(i):
        first, then = grad[:, columns(i)], res_ref[:, columns(i)]
        sol_ref[:, columns(i)] = alpha0 * first + alpha1 * (then + ratio * first)
        res_ref[:, columns(i)] = then - alpha1 * (
            image1[:, columns(i)] + ratio * image0[:, columns(i)]
        )

    drained(weights.at[pl.ds(0, n_unit * HALF)], d2d_send.at[0])
    slots = part1.shape[0]

    @pl.when(inner == 0)
    def _():
        drained(weights.at[pl.ds(0, subs * HALF)], in_send.at[0])
        for place, ref in enumerate((features, vector16, gated)):
            drained(ref, far_send.at[place])
        for sem in (rs_send1, ag_send1):
            drained(got1.at[pl.ds(0, n_unit - subs)], sem.at[0])

    @pl.when(inner == 1)
    def _():
        drained(weights.at[pl.ds(0, 2 * subs * HALF)], in_send.at[0])
        drained(weights.at[pl.ds(0, 3 * subs * HALF)], out_send.at[0])
        drained(far_image, far_send.at[3])
        for sem in (rs_send1, ag_send1):
            drained(got1.at[pl.ds(0, slots)], sem.at[0])

    every = pl.ds(0, n_chunk)
    drained(mixed2.at[every, pl.ds(0, 3)], rs_send2.at[0])
    drained(mixed2.at[every, pl.ds(0, 2)], ag_send2.at[0])
    drained(mixed2.at[every, 0], fw_send.at[0])
    for slot in range(2):
        drained(sums_got.at[slot], sum_send.at[slot])


def fused(n_tp, support_x, adapter_a, gate_pre, lengths, damping, down_w, grad_b):
    tokens, width = support_x.shape[1:]
    rank = adapter_a.shape[2]
    hidden, share = down_w.shape
    subs = share // HALF
    n_unit = 4 * subs
    slots = n_unit + subs
    rows = tokens // n_tp
    n_chunk = width // CHUNK
    tile = next(size for size in (512, 256, 128) if hidden % size == 0)
    f32, bf16 = jnp.float32, jnp.bfloat16
    dma = pltpu.SemaphoreType.DMA
    anywhere, vmem = pl.BlockSpec(memory_space=pl.ANY), pl.BlockSpec(memory_space=pltpu.VMEM)
    smem = pl.BlockSpec(memory_space=pltpu.SMEM)
    shape = jax.ShapeDtypeStruct((rank, hidden), f32)
    solved, residual = pl.pallas_call(
        kernel,
        out_shape=(shape, shape),
        in_specs=[anywhere, anywhere, anywhere, smem, smem, anywhere, anywhere],
        out_specs=(vmem, vmem),
        scratch_shapes=[
            pltpu.VMEM((tokens, width), bf16),
            pltpu.VMEM((rank, width), bf16),
            pltpu.VMEM((rank, hidden), f32),
            pltpu.VMEM((width, hidden), bf16),
            pltpu.VMEM((tokens, hidden), bf16),
            pltpu.VMEM((tokens, hidden), bf16),
            pltpu.VMEM((tokens, hidden), f32),
            pltpu.VMEM((tokens, rank), bf16),
            pltpu.VMEM((rank, hidden), f32),
            pltpu.VMEM((rank, hidden), f32),
            pltpu.VMEM((tokens, hidden), bf16),
            pltpu.VMEM((tokens, hidden), bf16),
            pltpu.VMEM((tokens, hidden), f32),
            pltpu.VMEM((tokens, rank), bf16),
            pltpu.VMEM((rank, hidden), bf16),
            pltpu.VMEM((rank, hidden), bf16),
            pltpu.VMEM((hidden // tile, rank, tile), bf16),
            pltpu.VMEM((hidden // tile, rank, tile), bf16),
            pltpu.VMEM((slots, n_tp, rows, UNIT), bf16),
            pltpu.VMEM((slots, n_tp - 1, rows, UNIT), bf16),
            pltpu.VMEM((slots, n_tp, rows, UNIT), bf16),
            pltpu.VMEM((n_chunk, n_tp, rows, CHUNK), bf16),
            pltpu.VMEM((n_chunk, 2, rows // 2, CHUNK), bf16),
            pltpu.VMEM((n_chunk, 2, rows // 2, CHUNK), bf16),
            pltpu.VMEM((n_chunk, 2, 2, rows // 2, CHUNK), bf16),
            pltpu.VMEM((n_chunk, n_tp, rows, CHUNK), bf16),
            pltpu.VMEM((2, 2, 8, 128), f32),
            pltpu.VMEM((2, n_tp - 1, 2, 8, 128), f32),
            dma((5,)),
            dma((n_unit,)),
            dma((n_unit,)),
            dma((1,)),
            dma((1,)),
            dma((1,)),
            dma((4,)),
            dma((4,)),
            dma((1,)),
            dma((slots,)),
            dma((1,)),
            dma((slots,)),
            dma((1,)),
            dma((n_chunk,)),
            dma((n_chunk,)),
            dma((1,)),
            dma((n_chunk,)),
            dma((1,)),
            dma((n_chunk,)),
            dma((2,)),
            dma((2,)),
        ],
        compiler_params=pltpu.CompilerParams(
            collective_id=0, has_side_effects=True, vmem_limit_bytes=66_000_000
        ),
    )(
        support_x[0], adapter_a[0].T, gate_pre[0], lengths, damping, down_w.T, grad_b[0]
    )
    return solved[None], residual[None]


def solution(mesh):
    in_specs = (
        P("task", None, None),
        P("task", None, None),
        P("task", None, "tp"),
        P("task"),
        P("task"),
        P("tp", "task"),
        P("task", None, "tp"),
    )
    out_specs = (P("task", None, "tp"), P("task", None, "tp"))
    n_task, n_tp = mesh.shape["task"], mesh.shape["tp"]

    def body(support_x, *rest):
        tokens, width = support_x.shape[1:]
        hidden, share = rest[4].shape
        even = tokens % (32 * n_tp) == 0 and hidden % 128 == 0
        if n_tp != 4 or n_task != 8 or share % HALF or width % CHUNK or not even:
            return shards(support_x, *rest)
        return fused(n_tp, support_x, *rest)

    return jax.shard_map(body, mesh=mesh, in_specs=in_specs, out_specs=out_specs, check_vma=False)
```

time: 256 us -> 294 us (1.15)
  Pallas kernels: 247 us -> 288 us
    pallas_call x1, Pallas kernels: 247 us -> 288 us  [fused(): pl.pallas_call(kernel, out_shape=(shape, shape), in_specs=[anywhere, anyw...]
    unnamed x3 -> x2, local copies, waits for them, and re-layouts: 6.2 us -> 3.94 us
where the time goes in v1:
time: 294 us
  Pallas kernels  288 us (98%)
  local copies, waits for them, and re-layouts  3.94 us (1%)
    pallas_call x1, Pallas kernels, fused(): pl.pallas_call(kernel, out_shape=(shape, shape), in_specs=[anywhere, anyw...  288 us

profile of v1, /device:TPU:0, one launch (start us, length us, event | category | flops | bytes accessed | tf_op | source)
XLA Modules:
  0.0 293.6 jit_solution(14625076495189059261)
XLA Ops:
  1.9 287.7 %shard_map.86 = (f32[64,2560]{1,0:T(8,128)}, f32[64,2560]{1,0:T(8,128)}) custom-call(bf16[384,3584]{1,0:T(8,128)(2,1)} %bitcast.9, bf16[64,3584]{1,0:T(8,128)(2,1)} %bitcast.15, bf16[384,2560]{1,0:T(8,128)(2,1)} %bitcast.11, s32[1]{0:T(128)S(6)} %copy.11.length_ref, f32[1]{0:T(128)S(6)} %copy.12.damping_ref, bf16[448,2560]{1,0:T(8,128)(2,1)} %bitcast.10, ...), custom_call_target="tpu_custom_call" | custom-call | tf_op jit(solution)/shard_map/pallas_call | solution.py:572
  289.6 2.0 copy.13
  291.6 2.0 copy.14

commit v2 on v1

--- a/solution.py
+++ b/solution.py
@@ -64,8 +64,9 @@
 HALF = 64
 UNIT = 2 * HALF
 CHUNK = 256
-AHEAD = 3
+AHEAD = 2
 EARLY = 3
+LAG = 3
 
 
 def arrival_order(subs):
@@ -91,7 +92,7 @@
 def kernel(
     support_hbm, adapter_hbm, gate_hbm, length_ref, damping_ref, w_hbm, grad_hbm,
     sol_ref, res_ref,
-    support, adapter, grad, weights, gated, active, total, features, image0, image1,
+    adapter, grad, weights, gated, active, total, features, image0, image1,
     far_gated, far_active, far_total, far_features, vector16, far_vector, far_image, image_got,
     part1, got1, mixed1, part2, pass2, added2, got2, mixed2, sums, sums_got,
     load_sem, w_recv, p_recv, in_send, out_send, d2d_send, far_send, far_recv,
@@ -142,8 +143,13 @@
     loads = [
         pltpu.make_async_copy(source, target, load_sem.at[1 + place])
         for place, (source, target) in enumerate(
-            ((gate_hbm, active), (support_hbm, support), (adapter_hbm, adapter), (grad_hbm, grad))
-        )
+            ((gate_hbm, active), (adapter_hbm, adapter), (grad_hbm, grad))
+        )
+    ] + [
+        pltpu.make_async_copy(
+            support_hbm.at[:, pl.ds(c * CHUNK, CHUNK)], part2.at[c], load_sem.at[4]
+        )
+        for c in range(n_chunk)
     ]
     for load in loads:
         load.start()
@@ -219,12 +225,16 @@
         share_half(first + s)
 
     loads[1].wait()
+    drained(part2, load_sem.at[4])
+    wide = jnp.zeros(features.shape, jnp.float32)
+    for c in range(n_chunk):
+        wide = wide + lax.dot_general(
+            part2[c], adapter[:, pl.ds(c * CHUNK, CHUNK)], (((1,), (1,)), ((), ())),
+            preferred_element_type=jnp.float32,
+        )
+    features[...] = wide.astype(jnp.bfloat16)
+    loads[0].wait()
     loads[2].wait()
-    features[...] = lax.dot_general(
-        support[...], adapter[...], (((1,), (1,)), ((), ())), preferred_element_type=jnp.float32
-    ).astype(jnp.bfloat16)
-    loads[0].wait()
-    loads[3].wait()
     live, rate = length_ref[0].astype(jnp.float32), damping_ref[0]
     positions = lax.broadcasted_iota(jnp.int32, (tokens, tile), 0).astype(jnp.float32)
 
@@ -291,13 +301,10 @@
 
     def back(slot, p, tot):
         drained(mixed1.at[slot, pl.ds(0, n_tp - 1)], ag_recv1.at[slot])
-        whole = mixed1[slot].reshape(tokens, UNIT)
-
-        @pl.loop(0, n_tile)
-        def _(i):
-            tot[:, columns(i)] += jnp.dot(
-                whole, weights[span(p), columns(i)], preferred_element_type=jnp.float32
-            )
+        tot[...] += jnp.dot(
+            mixed1[slot].reshape(tokens, UNIT), weights[span(p), :],
+            preferred_element_type=jnp.float32,
+        )
 
     def make_image(vector, image, slot, extra):
         def body(i, carry):
@@ -334,25 +341,25 @@
     make_active(features, vector16, gated, active, total)
     count = n_unit - subs + inner * subs
 
-    @pl.loop(0, count + 2)
+    @pl.loop(0, count + 2 * LAG)
     def _(e):
-        p, before, earlier = unit_of(e), unit_of(e - 1), unit_of(e - 2)
-
-        @pl.when((e >= 1) & (e <= count))
+        p, before, earlier = unit_of(e), unit_of(e - LAG), unit_of(e - 2 * LAG)
+
+        @pl.when((e >= LAG) & (e < count + LAG))
         def _():
-            reduce(e - 1)
-
             @pl.when(before >= 3 * subs)
             def _():
                 reduce(before + subs)
 
-        @pl.when(e >= 2)
+            reduce(e - LAG)
+
+        @pl.when(e >= 2 * LAG)
         def _():
             @pl.when(earlier >= 3 * subs)
             def _():
                 back(earlier + subs, earlier, far_total)
 
-            back(e - 2, earlier, total)
+            back(e - 2 * LAG, earlier, total)
 
         @pl.when(e < count)
         def _():
@@ -418,6 +425,10 @@
     beside, below = 2 * row + 1 - col, 2 * (1 - row) + col
     across = n_tp - 1 - j_me
     top, low = pl.ds(0, rows // 2), pl.ds(rows // 2, rows // 2)
+
+    def piece_rows(piece, place):
+        return pl.ds(pl.multiple_of(piece * rows + place * (rows // 2), 16), rows // 2)
+
     side, under = {"task": t_me, "tp": beside}, {"task": t_me, "tp": below}
     early = 3 * subs * UNIT // CHUNK
 
@@ -444,17 +455,17 @@
             active[...], weights[where, :], (((1,), (1,)), ((), ())),
             preferred_element_type=jnp.float32,
         )
-        part2[i] = partial_sum.astype(jnp.bfloat16).reshape(n_tp, rows, CHUNK)
-        push(part2.at[i, across, top], pass2.at[i, 0], rs_send2.at[0], pass_recv2.at[i], side)
-        push(part2.at[i, across, low], pass2.at[i, 1], rs_send2.at[0], pass_recv2.at[i], under)
-        push(part2.at[i, beside, top], got2.at[i, 0, 0], rs_send2.at[0], rs_recv2.at[i], side)
-        push(part2.at[i, below, low], got2.at[i, 1, 1], rs_send2.at[0], rs_recv2.at[i], under)
+        part2[i] = partial_sum.astype(jnp.bfloat16)
+        push(part2.at[i, piece_rows(across, 0)], pass2.at[i, 0], rs_send2.at[0], pass_recv2.at[i], side)
+        push(part2.at[i, piece_rows(across, 1)], pass2.at[i, 1], rs_send2.at[0], pass_recv2.at[i], under)
+        push(part2.at[i, piece_rows(beside, 0)], got2.at[i, 0, 0], rs_send2.at[0], rs_recv2.at[i], side)
+        push(part2.at[i, piece_rows(below, 1)], got2.at[i, 1, 1], rs_send2.at[0], rs_recv2.at[i], under)
 
     def relay(i):
         drained(pass2.at[i], pass_recv2.at[i])
-        for place, piece, where, target in ((0, below, top, under), (1, beside, low, side)):
+        for place, piece, target in ((0, below, under), (1, beside, side)):
             added2[i, place] = (
-                part2[i, piece, where].astype(jnp.float32) + pass2[i, place].astype(jnp.float32)
+                part2[i, piece_rows(piece, place)].astype(jnp.float32) + pass2[i, place].astype(jnp.float32)
             ).astype(jnp.bfloat16)
             push(
                 added2.at[i, place], got2.at[i, 1 - place, place],
@@ -465,7 +476,7 @@
         drained(got2.at[i], rs_recv2.at[i])
         for place, where in ((0, top), (1, low)):
             mixed2[i, j_me, where] = (
-                part2[i, j_me, where].astype(jnp.float32)
+                part2[i, piece_rows(j_me, place)].astype(jnp.float32)
                 + got2[i, 0, place].astype(jnp.float32)
                 + got2[i, 1, place].astype(jnp.float32)
             ).astype(jnp.bfloat16)
@@ -484,36 +495,52 @@
     def back2(i):
         _, where = stretch(i)
         drained(mixed2.at[i, 0], fw_recv.at[i])
-        whole = mixed2[i].reshape(tokens, CHUNK)
-
-        @pl.loop(0, n_tile)
-        def _(k):
-            total[:, columns(k)] += jnp.dot(
-                whole, weights[where, columns(k)], preferred_element_type=jnp.float32
-            )
-
-    for start, stop in ((0, early), (early, n_chunk)):
-        @pl.loop(start, stop)
-        def _(i):
-            product2(i)
-
-        @pl.loop(start, stop)
-        def _(i):
-            relay(i)
-
-        @pl.loop(start, stop)
-        def _(i):
-            reduce2(i)
-
-    @pl.loop(0, n_chunk + 2)
-    def _(i):
-        @pl.when(i < n_chunk)
-        def _():
-            forward2(i)
-
-        @pl.when(i >= 2)
-        def _():
-            back2(i - 2)
+        total[...] += jnp.dot(
+            mixed2[i].reshape(tokens, CHUNK), weights[where, :],
+            preferred_element_type=jnp.float32,
+        )
+
+    ready = early - (n_chunk - early)
+
+    @pl.loop(0, early)
+    def _(i):
+        product2(i)
+
+    @pl.loop(0, early)
+    def _(i):
+        relay(i)
+
+    @pl.loop(0, early)
+    def _(i):
+        reduce2(i)
+
+    @pl.loop(early, n_chunk)
+    def _(i):
+        product2(i)
+
+    @pl.loop(early, n_chunk)
+    def _(i):
+        relay(i)
+
+    @pl.loop(0, early)
+    def _(i):
+        forward2(i)
+
+    @pl.loop(early, n_chunk)
+    def _(i):
+        reduce2(i)
+
+    @pl.loop(0, ready)
+    def _(i):
+        back2(i)
+
+    @pl.loop(early, n_chunk)
+    def _(i):
+        forward2(i)
+
+    @pl.loop(ready, n_chunk)
+    def _(i):
+        back2(i)
 
     norm1, cross1 = make_image(res_ref, image1, 1, None)
     ratio = norm1 / norm0
@@ -575,7 +602,6 @@
         in_specs=[anywhere, anywhere, anywhere, smem, smem, anywhere, anywhere],
         out_specs=(vmem, vmem),
         scratch_shapes=[
-            pltpu.VMEM((tokens, width), bf16),
             pltpu.VMEM((rank, width), bf16),
             pltpu.VMEM((rank, hidden), f32),
             pltpu.VMEM((width, hidden), bf16),
@@ -596,7 +622,7 @@
             pltpu.VMEM((slots, n_tp, rows, UNIT), bf16),
             pltpu.VMEM((slots, n_tp - 1, rows, UNIT), bf16),
             pltpu.VMEM((slots, n_tp, rows, UNIT), bf16),
-            pltpu.VMEM((n_chunk, n_tp, rows, CHUNK), bf16),
+            pltpu.VMEM((n_chunk, tokens, CHUNK), bf16),
             pltpu.VMEM((n_chunk, 2, rows // 2, CHUNK), bf16),
             pltpu.VMEM((n_chunk, 2, rows // 2, CHUNK), bf16),
             pltpu.VMEM((n_chunk, 2, 2, rows // 2, CHUNK), bf16),

time: 294 us -> 210 us (0.71)
  Pallas kernels: 288 us -> 204 us
    pallas_call x1, Pallas kernels: 288 us -> 204 us  [fused(): pl.pallas_call(kernel, out_shape=(shape, shape), in_specs=[anywhere, anyw...]
where the time goes in v2:
time: 210 us; the launch traced here: 209 us
  Pallas kernels  204 us (97%)
  local copies, waits for them, and re-layouts  3.94 us (2%)
    pallas_call x1, Pallas kernels, fused(): pl.pallas_call(kernel, out_shape=(shape, shape), in_specs=[anywhere, anyw...  204 us

profile of v2, /device:TPU:0, one launch (start us, length us, event | category | flops | bytes accessed | tf_op | source)
XLA Modules:
  0.0 209.5 jit_solution(10392480078571315318)
XLA Ops:
  1.9 203.6 %shard_map.86 = (f32[64,2560]{1,0:T(8,128)}, f32[64,2560]{1,0:T(8,128)}) custom-call(bf16[384,3584]{1,0:T(8,128)(2,1)} %bitcast.9, bf16[64,3584]{1,0:T(8,128)(2,1)} %bitcast.15, bf16[384,2560]{1,0:T(8,128)(2,1)} %bitcast.11, s32[1]{0:T(128)S(6)} %copy.11.length_ref, f32[1]{0:T(128)S(6)} %copy.12.damping_ref, bf16[448,2560]{1,0:T(8,128)(2,1)} %bitcast.10, ...), custom_call_target="tpu_custom_call" | custom-call | tf_op jit(solution)/shard_map/pallas_call | solution.py:599
  205.5 2.0 copy.13
  207.5 2.0 copy.14

commit v3 on v2

--- a/solution.py
+++ b/solution.py
@@ -63,19 +63,19 @@
 MESH = pl.DeviceIdType.MESH
 HALF = 64
 UNIT = 2 * HALF
-CHUNK = 256
+PAIR = 2 * UNIT
+CHUNK = 512
 AHEAD = 2
 EARLY = 3
-LAG = 3
+LAG = 2
 
 
 def arrival_order(subs):
     near, far = list(range(subs)), list(range(subs - 1, -1, -1))
-    gate = subs
     clock, times = 0.0, []
     for place in near:
         if place == AHEAD:
-            clock += gate
+            clock += subs
         clock += 1.0
         times.append((clock, place))
     events = [(when, 0, place) for when, place in times]
@@ -86,7 +86,20 @@
         events.append((clock, 2, 3 * subs + far[place]))
     middle = [subs + place for place in near] + [unit for _, _, unit in sorted(events)]
     end = near + [subs + place for place in near] + [2 * subs + place for place in far]
-    return end + [0] * subs, middle
+    return [order if len(order) % 2 == 0 else order + order[-1:] for order in (end, middle)]
+
+
+def far_pairs(order, subs):
+    pairs, held, slots = [], [], len(order) // 2
+    for e in range(slots):
+        held += [unit for unit in order[2 * e : 2 * e + 2] if unit >= 3 * subs]
+        take = []
+        if len(held) >= 2:
+            take = [held.pop(0), held.pop(0)]
+        elif held and e >= slots - 2:
+            take = [held[0], held.pop(0)]
+        pairs.append(take)
+    return pairs
 
 
 def kernel(
@@ -112,14 +125,35 @@
     n_chunk = part2.shape[0]
     tile = far_image.shape[2]
     n_tile = hidden // tile
-    orders = arrival_order(subs)
-
-    def unit_of(e):
-        unit = orders[0][0] + inner * (orders[1][0] - orders[0][0])
-        for place in range(1, n_unit):
-            first, second = orders[0][place], orders[1][place]
-            unit = jnp.where(e == place, first + inner * (second - first), unit)
-        return unit
+    ends, middles = arrival_order(subs)
+    fars = far_pairs(middles, subs)
+    n_far = sum(1 for pair in fars if pair)
+    numbers = [sum(1 for pair in fars[:e] if pair) for e in range(len(fars))]
+    slots = len(fars)
+
+    def pick(e, table):
+        value = table[0]
+        for place in range(1, slots):
+            if place < len(table):
+                value = jnp.where(e == place, table[place], value)
+        return value
+
+    def pair_of(e):
+        found = []
+        for k in range(2):
+            first, second = ends[k::2], middles[k::2]
+            first = first + first[-1:] * (slots - len(first))
+            found.append(pick(e, [f + inner * (g - f) for f, g in zip(first, second)]))
+        return found
+
+    def far_of(e):
+        return [pick(e, [pair[k] if pair else 0 for pair in fars]) for k in range(2)]
+
+    def far_slot(e):
+        return slots + pick(e, numbers)
+
+    def has_far(e):
+        return (inner == 1) & (pick(e, [1 if pair else 0 for pair in fars]) == 1)
 
     def placed(p):
         return p + upper * (n_unit - 1 - 2 * p)
@@ -241,7 +275,7 @@
     def columns(i):
         return pl.ds(pl.multiple_of(i * tile, tile), tile)
 
-    @pl.loop(0, n_tile)
+    @pl.loop(0, n_tile, unroll=True)
     def _(i):
         pre = active[:, columns(i)].astype(jnp.float32)
         gated[:, columns(i)] = jnp.where(
@@ -265,7 +299,7 @@
         image_got[...] = jnp.zeros_like(image_got)
 
     def make_active(feats, vector, gate, act, tot):
-        @pl.loop(0, n_tile)
+        @pl.loop(0, n_tile, unroll=True)
         def _(i):
             wide = jnp.dot(
                 feats[...], vector[:, columns(i)], preferred_element_type=jnp.float32
@@ -275,12 +309,18 @@
             )
             tot[:, columns(i)] = jnp.zeros_like(wide)
 
-    def product(slot, p, act):
+    def pair_rows(pair):
+        return jnp.concatenate([weights[span(pair[0]), :], weights[span(pair[1]), :]], axis=0)
+
+    def product(slot, pair, act):
         partial_sum = lax.dot_general(
-            act[...], weights[span(p), :], (((1,), (1,)), ((), ())),
+            act[...], pair_rows(pair), (((1,), (1,)), ((), ())),
             preferred_element_type=jnp.float32,
         )
-        part1[slot] = partial_sum.astype(jnp.bfloat16).reshape(n_tp, rows, UNIT)
+        lanes = lax.broadcasted_iota(jnp.int32, partial_sum.shape, 1)
+        kept = jnp.where(pair[0] == pair[1], UNIT, PAIR)
+        partial_sum = jnp.where(lanes < kept, partial_sum, 0.0)
+        part1[slot] = partial_sum.astype(jnp.bfloat16).reshape(n_tp, rows, PAIR)
         for d in range(1, n_tp):
             push(
                 part1.at[slot, lax.rem(j_me + d, n_tp)], got1.at[slot, d - 1],
@@ -299,10 +339,10 @@
                 ag_send1.at[0], ag_recv1.at[slot], peer,
             )
 
-    def back(slot, p, tot):
+    def back(slot, pair, tot):
         drained(mixed1.at[slot, pl.ds(0, n_tp - 1)], ag_recv1.at[slot])
         tot[...] += jnp.dot(
-            mixed1[slot].reshape(tokens, UNIT), weights[span(p), :],
+            mixed1[slot].reshape(tokens, PAIR), pair_rows(pair),
             preferred_element_type=jnp.float32,
         )
 
@@ -323,7 +363,7 @@
             return carry[0] + v * v, carry[1] + v * value
 
         zero = jnp.zeros((vector.shape[0], tile), jnp.float32)
-        squares, crosses = lax.fori_loop(0, n_tile, body, (zero, zero))
+        squares, crosses = lax.fori_loop(0, n_tile, body, (zero, zero), unroll=True)
         sums[slot, 0] = jnp.broadcast_to(jnp.sum(squares, keepdims=True), (8, 128))
         sums[slot, 1] = jnp.broadcast_to(jnp.sum(crosses, keepdims=True), (8, 128))
         for d in range(1, n_tp):
@@ -339,51 +379,57 @@
         return norm, cross
 
     make_active(features, vector16, gated, active, total)
-    count = n_unit - subs + inner * subs
+    short = len(ends) // 2
+    count = short + inner * (slots - short)
 
     @pl.loop(0, count + 2 * LAG)
     def _(e):
-        p, before, earlier = unit_of(e), unit_of(e - LAG), unit_of(e - 2 * LAG)
-
         @pl.when((e >= LAG) & (e < count + LAG))
         def _():
-            @pl.when(before >= 3 * subs)
+            @pl.when(has_far(e - LAG))
             def _():
-                reduce(before + subs)
+                reduce(far_slot(e - LAG))
 
             reduce(e - LAG)
 
         @pl.when(e >= 2 * LAG)
         def _():
-            @pl.when(earlier >= 3 * subs)
+            @pl.when(has_far(e - 2 * LAG))
             def _():
-                back(earlier + subs, earlier, far_total)
-
-            back(e - 2 * LAG, earlier, total)
+                back(far_slot(e - 2 * LAG), far_of(e - 2 * LAG), far_total)
+
+            @pl.when(e < count)
+            def _():
+                back(e - 2 * LAG, pair_of(e - 2 * LAG), total)
 
         @pl.when(e < count)
         def _():
-            @pl.when(e >= subs)
+            pair = pair_of(e)
+            for k, p in enumerate(pair):
+                @pl.when((2 * e + k >= subs) & ((k == 0) | (pair[0] != pair[1])))
+                def _(p=p):
+                    arrive(p)
+
+            for k, p in enumerate(pair):
+                @pl.when((k == 0) | (pair[0] != pair[1]))
+                def _(p=p):
+                    completed(p)
+
+            @pl.when(has_far(e))
             def _():
-                arrive(p)
-
-            completed(p)
-
-            @pl.when(p >= 3 * subs)
-            def _():
-                @pl.when(p == n_unit - 1)
+                @pl.when(far_slot(e) == slots)
                 def _():
                     for place, ref in enumerate((far_features, far_vector, far_gated)):
                         drained(ref, far_recv.at[place])
                     make_active(far_features, far_vector, far_gated, far_active, far_total)
 
-                product(p + subs, p, far_active)
-
-            product(e, p, active)
+                product(far_slot(e), far_of(e), far_active)
+
+            product(e, pair, active)
 
     @pl.when(inner == 1)
     def _():
-        @pl.loop(0, n_tile)
+        @pl.loop(0, n_tile, unroll=True)
         def _(i):
             second = (
                 far_gated[:, columns(i)].astype(jnp.float32) * far_total[:, columns(i)]
@@ -398,6 +444,10 @@
         def _(s):
             send_half(n_unit - 1 - EARLY - s, outward, out_send)
 
+    @pl.loop(count - 2 * LAG, count)
+    def _(e):
+        back(e, pair_of(e), total)
+
     @pl.when(inner == 0)
     def _():
         @pl.loop(0, EARLY)
@@ -409,7 +459,7 @@
     norm0, cross0 = make_image(grad, image0, 0, image_got)
     alpha0 = norm0 / cross0
 
-    @pl.loop(0, n_tile)
+    @pl.loop(0, n_tile, unroll=True)
     def _(i):
         value = grad[:, columns(i)] - alpha0 * image0[:, columns(i)]
         res_ref[:, columns(i)] = value
@@ -442,7 +492,9 @@
 
         @pl.when((inner == 0) & (i >= early))
         def _():
-            for p in (2 * c + 1, 2 * c):
+            for k in range(CHUNK // UNIT - 1, -1, -1):
+                p = CHUNK // UNIT * c + k
+
                 @pl.when(p >= 3 * subs)
                 def _(p=p):
                     @pl.when(p < n_unit - EARLY)
@@ -546,7 +598,7 @@
     ratio = norm1 / norm0
     alpha1 = norm1 / (cross1 - ratio * norm1 / alpha0)
 
-    @pl.loop(0, n_tile)
+    @pl.loop(0, n_tile, unroll=True)
     def _(i):
         first, then = grad[:, columns(i)], res_ref[:, columns(i)]
         sol_ref[:, columns(i)] = alpha0 * first + alpha1 * (then + ratio * first)
@@ -555,7 +607,6 @@
         )
 
     drained(weights.at[pl.ds(0, n_unit * HALF)], d2d_send.at[0])
-    slots = part1.shape[0]
 
     @pl.when(inner == 0)
     def _():
@@ -563,7 +614,7 @@
         for place, ref in enumerate((features, vector16, gated)):
             drained(ref, far_send.at[place])
         for sem in (rs_send1, ag_send1):
-            drained(got1.at[pl.ds(0, n_unit - subs)], sem.at[0])
+            drained(got1.at[pl.ds(0, short)], sem.at[0])
 
     @pl.when(inner == 1)
     def _():
@@ -571,7 +622,7 @@
         drained(weights.at[pl.ds(0, 3 * subs * HALF)], out_send.at[0])
         drained(far_image, far_send.at[3])
         for sem in (rs_send1, ag_send1):
-            drained(got1.at[pl.ds(0, slots)], sem.at[0])
+            drained(got1.at[pl.ds(0, slots + n_far)], sem.at[0])
 
     every = pl.ds(0, n_chunk)
     drained(mixed2.at[every, pl.ds(0, 3)], rs_send2.at[0])
@@ -587,7 +638,8 @@
     hidden, share = down_w.shape
     subs = share // HALF
     n_unit = 4 * subs
-    slots = n_unit + subs
+    middle = arrival_order(subs)[1]
+    slots = len(middle) // 2 + sum(1 for pair in far_pairs(middle, subs) if pair)
     rows = tokens // n_tp
     n_chunk = width // CHUNK
     tile = next(size for size in (512, 256, 128) if hidden % size == 0)
@@ -619,9 +671,9 @@
             pltpu.VMEM((rank, hidden), bf16),
             pltpu.VMEM((hidden // tile, rank, tile), bf16),
             pltpu.VMEM((hidden // tile, rank, tile), bf16),
-            pltpu.VMEM((slots, n_tp, rows, UNIT), bf16),
-            pltpu.VMEM((slots, n_tp - 1, rows, UNIT), bf16),
-            pltpu.VMEM((slots, n_tp, rows, UNIT), bf16),
+            pltpu.VMEM((slots, n_tp, rows, PAIR), bf16),
+            pltpu.VMEM((slots, n_tp - 1, rows, PAIR), bf16),
+            pltpu.VMEM((slots, n_tp, rows, PAIR), bf16),
             pltpu.VMEM((n_chunk, tokens, CHUNK), bf16),
             pltpu.VMEM((n_chunk, 2, rows // 2, CHUNK), bf16),
             pltpu.VMEM((n_chunk, 2, rows // 2, CHUNK), bf16),

time: 210 us -> 205 us (0.976)
  Pallas kernels: 204 us -> 199 us
    pallas_call x1, Pallas kernels: 204 us -> 199 us  [fused(): pl.pallas_call(kernel, out_shape=(shape, shape), in_specs=[anywhere, anyw...]
where the time goes in v3:
time: 205 us
  Pallas kernels  199 us (97%)
  local copies, waits for them, and re-layouts  3.94 us (2%)
    pallas_call x1, Pallas kernels, fused(): pl.pallas_call(kernel, out_shape=(shape, shape), in_specs=[anywhere, anyw...  199 us

profile of v3, /device:TPU:0, one launch (start us, length us, event | category | flops | bytes accessed | tf_op | source)
XLA Modules:
  0.0 205.2 jit_solution(8878072128073326504)
XLA Ops:
  1.9 199.4 %shard_map.86 = (f32[64,2560]{1,0:T(8,128)}, f32[64,2560]{1,0:T(8,128)}) custom-call(bf16[384,3584]{1,0:T(8,128)(2,1)} %bitcast.9, bf16[64,3584]{1,0:T(8,128)(2,1)} %bitcast.15, bf16[384,2560]{1,0:T(8,128)(2,1)} %bitcast.11, s32[1]{0:T(128)S(6)} %copy.11.length_ref, f32[1]{0:T(128)S(6)} %copy.12.damping_ref, bf16[448,2560]{1,0:T(8,128)(2,1)} %bitcast.10, ...), custom_call_target="tpu_custom_call" | custom-call | tf_op jit(solution)/shard_map/pallas_call | solution.py:651
  201.3 2.0 copy.13
  203.3 2.0 copy.14

commit v4 on v3

--- a/solution.py
+++ b/solution.py
@@ -630,6 +630,11 @@
     drained(mixed2.at[every, 0], fw_send.at[0])
     for slot in range(2):
         drained(sums_got.at[slot], sum_send.at[slot])
+
+
+def settle(first, second, first_out, second_out):
+    first_out[...] = first[...]
+    second_out[...] = second[...]
 
 
 def fused(n_tp, support_x, adapter_a, gate_pre, lengths, damping, down_w, grad_b):
@@ -709,6 +714,12 @@
     )(
         support_x[0], adapter_a[0].T, gate_pre[0], lengths, damping, down_w.T, grad_b[0]
     )
+    solved, residual = pl.pallas_call(
+        settle,
+        out_shape=(shape, shape),
+        in_specs=[vmem, vmem],
+        out_specs=(vmem, vmem),
+    )(solved, residual)
     return solved[None], residual[None]
 
 

time: 205 us -> 204 us (level)
  local copies, waits for them, and re-layouts: 3.94 us -> 0 us
  Pallas kernels: 199 us -> 202 us
    unnamed x2 -> x0, local copies, waits for them, and re-layouts: 3.94 us -> none
    pallas_call x0 -> x1, Pallas kernels: none -> 2.38 us  [fused(): pl.pallas_call(settle, out_shape=(shape, shape), in_specs=[vmem, vmem], o...]
where the time goes in v4:
time: 204 us
  Pallas kernels  202 us (99%)
    pallas_call x1, Pallas kernels, fused(): pl.pallas_call(kernel, out_shape=(shape, shape), in_specs=[anywhere, anyw...  199 us

profile of v4, /device:TPU:0, one launch (start us, length us, event | category | flops | bytes accessed | tf_op | source)
XLA Modules:
  0.0 203.7 jit_solution(5827290434733472993)
XLA Ops:
  1.9 199.4 %shard_map.86 = (f32[64,2560]{1,0:T(8,128)}, f32[64,2560]{1,0:T(8,128)}) custom-call(bf16[384,3584]{1,0:T(8,128)(2,1)} %bitcast.9, bf16[64,3584]{1,0:T(8,128)(2,1)} %bitcast.13, bf16[384,2560]{1,0:T(8,128)(2,1)} %bitcast.11, s32[1]{0:T(128)S(6)} %copy.9.length_ref, f32[1]{0:T(128)S(6)} %copy.10.damping_ref, bf16[448,2560]{1,0:T(8,128)(2,1)} %bitcast.10, ...), custom_call_target="tpu_custom_call" | custom-call | tf_op jit(solution)/shard_map/pallas_call | solution.py:656
  201.3 2.4 %shard_map.87 = (f32[64,2560]{1,0:T(8,128)}, f32[64,2560]{1,0:T(8,128)}) custom-call(f32[64,2560]{1,0:T(8,128)} %get-tuple-element.6.first, f32[64,2560]{1,0:T(8,128)} %get-tuple-element.7.second), custom_call_target="tpu_custom_call" | custom-call | tf_op jit(solution)/shard_map/pallas_call | solution.py:717
